TPU v7x, 256 devices: a whole 4x4x8 slice. The times are simulated.
256 devices in a mesh: grp: 8 (over z), sp: 32 (over y, x, core).
Axes of the slice: x: 4, y: 4, z: 8, core: 2. Of those that a mesh axis runs over, the one named last changes fastest.
Arguments:
- tokens: bfloat16 [16384, 2880], P(('grp', 'sp')), may hold values from -36 to 36
- query_weight: bfloat16 [2880, 2048], P(None, 'sp'), may hold values from -0.109375 to 0.109375
- key_value_weight: bfloat16 [2880, 1024], replicated, may hold values from -0.109375 to 0.109375
- block_places: int32 [32], replicated, may hold values from 0 to 31, each once
- sinks: float32 [32], replicated, may hold values from -1 to 5
Outputs:
- attended: bfloat16 [16384, 2048], P(('grp', 'sp'))
Inputs may be any that keep to these rules, and one draw needn't show every extreme that they name: `block_places`: every sequence block appears once.
All inputs are finite; a program needn't handle non-finite values.
Results may differ from a plain program's by a relative error of at most 0.008.
The roundings to bfloat16 on the way count: a program that leaves them out, or rounds other values in their place, can miss the bound.
Values may be sent and summed in bfloat16 or wider, within the bound.
A program may use at most 128 MiB of HBM per device.

v0:
```python
import jax
import jax.numpy as jnp
from jax import lax
from jax.sharding import PartitionSpec as P

QUERY_HEADS = 32
HEAD_SIZE = 64
BPG = 4
rope_base = 150000.0
neg_large = -1e30


def joined_along(pieces, dim):
    pieces = jnp.moveaxis(pieces, 0, dim)
    shape = pieces.shape
    return pieces.reshape(*shape[:dim], shape[dim] * shape[dim + 1], *shape[dim + 2 :])


def piecewise(value, axis, dim, apply, out_dim):
    size, span = (lax.axis_size(axis), value.shape[dim])
    count = 2 if span % 2 == 0 else 1
    finished, length = ([], span // count)
    for k in range(count):
        share = lax.slice_in_dim(value, k * length, (k + 1) * length, axis=dim)
        starts = jnp.arange(size) * span + k * length
        finished.append(jax.vmap(apply)(lax.all_gather(share, axis), starts))
    return joined_along(jnp.concatenate(finished, axis=out_dim + 1), out_dim)


def rotate(vectors, angles):
    middle = vectors.shape[-1] // 2
    first_half = vectors[..., :middle]
    second_half = vectors[..., middle:]
    cosine = jnp.cos(angles)
    sine_part = jnp.sin(angles)
    return jnp.concatenate(
        [
            first_half * cosine - second_half * sine_part,
            second_half * cosine + first_half * sine_part,
        ],
        axis=-1,
    )


def locate(stored, block_rows, block_places):
    blocks = stored // block_rows
    table = jnp.arange(block_places.shape[0], dtype=jnp.int32)
    onehot = (blocks[:, None] == table[None, :]).astype(jnp.int32)
    return jnp.sum(onehot * block_places[None, :], axis=1) * block_rows + stored % block_rows


def prepare(projected, own_places, query_cols, kv_cols, head_count):
    row_count = projected.shape[0]
    inverse = rope_base ** (-(jnp.arange(HEAD_SIZE // 2, dtype=jnp.float32) * 2.0) / HEAD_SIZE)
    angles = own_places.astype(jnp.float32)[:, None, None] * inverse[None, None, :]
    queries = rotate(
        projected[:, :query_cols].reshape(row_count, query_cols // HEAD_SIZE, HEAD_SIZE), angles
    ).astype(jnp.bfloat16)
    rotated_keys = rotate(
        projected[:, query_cols : query_cols + kv_cols].reshape(row_count, head_count, HEAD_SIZE),
        angles,
    )
    key_value_pair = jnp.concatenate(
        [rotated_keys.reshape(row_count, kv_cols), projected[:, query_cols + kv_cols :]], axis=1
    ).astype(jnp.bfloat16)
    return (queries, key_value_pair)


def attend(state, queries, query_places, key_value_pair, key_places, head_count):
    maxima, totals, mixture = state
    key_count = key_value_pair.shape[0]
    column_half = key_value_pair.shape[1] // 2
    key_part = key_value_pair[:, :column_half].reshape(key_count, head_count, HEAD_SIZE)
    value_part = key_value_pair[:, column_half:].reshape(key_count, head_count, HEAD_SIZE)
    scores = jnp.einsum(
        "qhgd,khd->hgqk", queries, key_part, preferred_element_type=jnp.float32
    ) * HEAD_SIZE ** (-0.5)
    allowed = key_places[None, :] <= query_places[:, None]
    scores = jnp.where(allowed, scores, neg_large)
    updated = jnp.maximum(maxima, jnp.max(scores, axis=-1))
    weights = jnp.where(allowed, jnp.exp(scores - updated[..., None]), 0.0)
    factor = jnp.exp(maxima - updated)
    totals = totals * factor + jnp.sum(weights, axis=-1)
    mixture = mixture * factor[..., None] + jnp.einsum(
        "hgqk,khd->hgqd",
        weights.astype(jnp.bfloat16),
        value_part,
        preferred_element_type=jnp.float32,
    )
    return (updated, totals, mixture)


def per_device(tokens, query_weight, key_value_weight, block_places, sinks):
    sp_count = lax.axis_size("sp")
    local_rows = tokens.shape[0]
    group_rows = local_rows * sp_count
    block_rows = group_rows // BPG
    kv_total = key_value_weight.shape[1] // (2 * HEAD_SIZE)
    sp_place = lax.axis_index("sp")
    grp_place = lax.axis_index("grp")
    query_cols = query_weight.shape[1]
    query_heads = query_cols // HEAD_SIZE
    head_count = max(kv_total // sp_count, 1)
    kv_cols = head_count * HEAD_SIZE
    first_head = sp_place * query_heads // (QUERY_HEADS // kv_total)
    key_weight = lax.dynamic_slice_in_dim(key_value_weight, first_head * HEAD_SIZE, kv_cols, 1)
    value_weight = lax.dynamic_slice_in_dim(
        key_value_weight, kv_total * HEAD_SIZE + first_head * HEAD_SIZE, kv_cols, 1
    )
    joined = jnp.concatenate([query_weight, key_weight, value_weight], axis=1)

    def project(piece, start):
        return jnp.dot(piece, joined, preferred_element_type=jnp.float32)

    projected = piecewise(tokens, "sp", 0, project, 0)
    query_local = jnp.arange(group_rows, dtype=jnp.int32)
    head_first = sp_place * query_heads
    own_places = locate(grp_place * group_rows + query_local, block_rows, block_places)
    queries, key_value_pair = prepare(projected, own_places, query_cols, kv_cols, head_count)
    query_sharing = query_heads // head_count
    head_sinks = lax.dynamic_slice_in_dim(sinks, head_first, query_heads, 0).reshape(
        head_count, query_sharing
    )
    sink_rows = jnp.broadcast_to(head_sinks[:, :, None], (head_count, query_sharing, group_rows))
    query_block4 = queries.reshape(group_rows, head_count, query_sharing, HEAD_SIZE)
    initial = (
        sink_rows,
        jnp.ones((head_count, query_sharing, group_rows), jnp.float32),
        jnp.zeros((head_count, query_sharing, group_rows, HEAD_SIZE), jnp.float32),
    )
    piece = lax.all_gather(key_value_pair, "grp", axis=0, tiled=True)
    step_rows = min(piece.shape[0], group_rows)
    turns = piece.shape[0] // step_rows

    def visit(turn, inner):
        offset = turn * step_rows
        piece_rows = lax.dynamic_slice_in_dim(piece, offset, step_rows, 0)
        position = offset + jnp.arange(step_rows, dtype=jnp.int32)
        stored = position // group_rows * group_rows + position % group_rows
        key_places = locate(stored, block_rows, block_places)
        return attend(inner, query_block4, own_places, piece_rows, key_places, head_count)

    maxima, totals, mixture = lax.fori_loop(0, turns, visit, initial)
    normed = jnp.transpose(mixture, (2, 0, 1, 3)) / jnp.transpose(totals, (2, 0, 1))[..., None]
    attended = normed.reshape(group_rows, query_cols).astype(jnp.bfloat16)
    return lax.all_to_all(attended, "sp", split_axis=0, concat_axis=1, tiled=True)


def solution(mesh):
    in_specs = (P(("grp", "sp"), None), P(None, "sp"), P(), P(), P())
    out_specs = P(("grp", "sp"), None)
    return jax.shard_map(
        per_device, mesh=mesh, in_specs=in_specs, out_specs=out_specs, check_vma=False
    )
```

profile of v0, /device:TPU:1, one launch (start us, length us, event | category | flops | bytes accessed | tf_op | source)
XLA Modules:
  0.0 353.2 jit_solution(3869679549317436455)
XLA Ops:
  11.8 55.8 %all-gather.8.cloned.1.call-done = bf16[1024,2880]{1,0:T(8,128)(2,1)} async-done(((bf16[32,2880]{1,0:T(8,128)(2,1)}), bf16[1024,2880]{1,0:T(8,128)(2,1)}) %all-gather.8.cloned.1.call-update) | async-done | bytes 5898256 | tf_op jit(solution)/shard_map/all_gather | solution.py:26
  67.6 4.5 %convolution_bitcast_fusion.1 = f32[32,32,192]{2,1,0:T(8,128)S(1)} fusion(bf16[32,32,2880]{2,1,0:T(8,128)(2,1)} %bitcast.94, bf16[2880,64]{0,1:T(8,128)(2,1)S(1)} %copy.44, bf16[2880,64]{0,1:T(8,128)(2,1)S(1)} %copy.43, bf16[2880,64]{0,1:T(8,128)(2,1)S(1)} %copy-done.2), kind=kOutput, calls=%fused_computation.49 | convolution fusion | flops 1135779840 | bytes 7790592 | tf_op jit(solution)/shard_map/vmap()/dot_general | solution.py:113
  72.1 50.5 %all-gather.10.cloned.1.call-done = bf16[1024,2880]{1,0:T(8,128)(2,1)} async-done(((bf16[32,2880]{1,0:T(8,128)(2,1)}), bf16[1024,2880]{1,0:T(8,128)(2,1)}) %all-gather.10.cloned.1.call-update) | async-done | bytes 5898256 | tf_op jit(solution)/shard_map/all_gather | solution.py:26
  122.6 4.5 %convolution_bitcast_fusion = f32[32,32,192]{2,1,0:T(8,128)S(1)} fusion(bf16[32,32,2880]{2,1,0:T(8,128)(2,1)} %bitcast.95, bf16[2880,64]{0,1:T(8,128)(2,1)S(1)} %copy.44, bf16[2880,64]{0,1:T(8,128)(2,1)S(1)} %copy.43, bf16[2880,64]{0,1:T(8,128)(2,1)S(1)} %copy-done.2), kind=kOutput, calls=%fused_computation.48 | convolution fusion | flops 1135779840 | bytes 7790592 | tf_op jit(solution)/shard_map/vmap()/dot_general | solution.py:113
  131.3 52.6 %all-gather.6.cloned.1.call-done = bf16[16384,128]{0,1:T(8,128)(2,1)} async-done(((bf16[2048,128]{0,1:T(8,128)(2,1)}), bf16[16384,128]{0,1:T(8,128)(2,1)}) %all-gather.6.cloned.1.call-update) | async-done | bytes 4194320 | tf_op jit(solution)/shard_map/all_gather | solution.py:131
  184.5 141.5 %while.21 = (s32[]{:T(128)}, f32[1,1,2048]{2,1,0:T(1,128)S(1)}, f32[1,1,2048]{2,1,0:T(1,128)S(1)}, f32[1,1,2048,64]{2,3,1,0:T(8,128)S(1)}, s32[32]{0:T(128)S(1)}...) while((s32[]{:T(128)}, f32[1,1,2048]{2,1,0:T(1,128)S(1)}, ...), condition=%wide.region_5.6_spmd.clone, body=%wide.region_1.5_spmd.clone.sunk | while | flops 1141592064 | bytes 119497064 | solution.py:143
  188.3 5.3 %fusion.75 = f32[2048]{0:T(1024)S(1)} fusion(f32[2048,2048]{1,0:T(8,128)S(1)} %get-tuple-element.393, f32[2048]{0:T(1024)S(1)} %bitcast.86, s32[2048]{0:T(1024)S(1)} %get-tuple-element.427, s32[2048]{0:T(1024)S(1)} %fusion.73), kind=kLoop, calls=%fused_computation.4.clone.1 | loop fusion | flops 25163776 | bytes 16809984 | tf_op jit(solution)/shard_map/while/body/eval_jaxpr/reduce_sum | solution.py:83
  194.1 8.1 %fusion.77 = f32[1,1,2048,64]{2,3,1,0:T(8,128)S(1)} fusion(f32[2048,2048]{1,0:T(8,128)} %copy-done, f32[2048]{0:T(1024)S(1)} %bitcast.87, s32[2048]{0:T(1024)S(1)} %get-tuple-element.427, s32[2048]{0:T(1024)S(1)} %fusion.73, f32[1,1,2048,64]{2,3,1,0:T(8,128)S(1)} %get-tuple-element.412, bf16[16384,128]{0,1:T(8,128)(2,1)} %get-tuple-element.428, ...), kind=kOutput, calls=%fused_computation.8.clone.1 | convolution fusion | flops 562429952 | bytes 18120712 | tf_op jit(solution)/shard_map/while/body/eval_jaxpr/hgqk,khd->hgqd/dot_general | solution.py:84
  202.4 3.6 %fusion.74 = (f32[2048]{0:T(1024)S(1)}, f32[2048,2048]{1,0:T(8,128)S(1)}) fusion(s32[2048]{0:T(1024)S(1)} %get-tuple-element.427, s32[2048]{0:T(1024)S(1)} %fusion.73, bf16[2048,1,1,64]{0,3,2,1:T(8,128)(2,1)S(1)} %get-tuple-element.429, bf16[16384,128]{0,1:T(8,128)(2,1)} %get-tuple-element.428, s32[]{:T(128)S(6)} %select_n.248), kind=kOutput, calls=%fused_computation.2.clone.1 | convolution fusion | flops 553646080 | bytes 17326084 | tf_op jit(solution)/shard_map/while/body/eval_jaxpr/qhgd,khd->hgqk/dot_general | solution.py:75
  206.0 5.3 %fusion.75 = f32[2048]{0:T(1024)S(1)} fusion(f32[2048,2048]{1,0:T(8,128)S(1)} %get-tuple-element.393, f32[2048]{0:T(1024)S(1)} %bitcast.86, s32[2048]{0:T(1024)S(1)} %get-tuple-element.427, s32[2048]{0:T(1024)S(1)} %fusion.73), kind=kLoop, calls=%fused_computation.4.clone.1 | loop fusion | flops 25163776 | bytes 16809984 | tf_op jit(solution)/shard_map/while/body/eval_jaxpr/reduce_sum | solution.py:83
  211.8 8.1 %fusion.77 = f32[1,1,2048,64]{2,3,1,0:T(8,128)S(1)} fusion(f32[2048,2048]{1,0:T(8,128)} %copy-done, f32[2048]{0:T(1024)S(1)} %bitcast.87, s32[2048]{0:T(1024)S(1)} %get-tuple-element.427, s32[2048]{0:T(1024)S(1)} %fusion.73, f32[1,1,2048,64]{2,3,1,0:T(8,128)S(1)} %get-tuple-element.412, bf16[16384,128]{0,1:T(8,128)(2,1)} %get-tuple-element.428, ...), kind=kOutput, calls=%fused_computation.8.clone.1 | convolution fusion | flops 562429952 | bytes 18120712 | tf_op jit(solution)/shard_map/while/body/eval_jaxpr/hgqk,khd->hgqd/dot_general | solution.py:84
  223.7 5.3 %fusion.75 = f32[2048]{0:T(1024)S(1)} fusion(f32[2048,2048]{1,0:T(8,128)S(1)} %get-tuple-element.393, f32[2048]{0:T(1024)S(1)} %bitcast.86, s32[2048]{0:T(1024)S(1)} %get-tuple-element.427, s32[2048]{0:T(1024)S(1)} %fusion.73), kind=kLoop, calls=%fused_computation.4.clone.1 | loop fusion | flops 25163776 | bytes 16809984 | tf_op jit(solution)/shard_map/while/body/eval_jaxpr/reduce_sum | solution.py:83
  229.5 8.1 %fusion.77 = f32[1,1,2048,64]{2,3,1,0:T(8,128)S(1)} fusion(f32[2048,2048]{1,0:T(8,128)} %copy-done, f32[2048]{0:T(1024)S(1)} %bitcast.87, s32[2048]{0:T(1024)S(1)} %get-tuple-element.427, s32[2048]{0:T(1024)S(1)} %fusion.73, f32[1,1,2048,64]{2,3,1,0:T(8,128)S(1)} %get-tuple-element.412, bf16[16384,128]{0,1:T(8,128)(2,1)} %get-tuple-element.428, ...), kind=kOutput, calls=%fused_computation.8.clone.1 | convolution fusion | flops 562429952 | bytes 18120712 | tf_op jit(solution)/shard_map/while/body/eval_jaxpr/hgqk,khd->hgqd/dot_general | solution.py:84
  241.4 5.3 %fusion.75 = f32[2048]{0:T(1024)S(1)} fusion(f32[2048,2048]{1,0:T(8,128)S(1)} %get-tuple-element.393, f32[2048]{0:T(1024)S(1)} %bitcast.86, s32[2048]{0:T(1024)S(1)} %get-tuple-element.427, s32[2048]{0:T(1024)S(1)} %fusion.73), kind=kLoop, calls=%fused_computation.4.clone.1 | loop fusion | flops 25163776 | bytes 16809984 | tf_op jit(solution)/shard_map/while/body/eval_jaxpr/reduce_sum | solution.py:83
  247.1 8.1 %fusion.77 = f32[1,1,2048,64]{2,3,1,0:T(8,128)S(1)} fusion(f32[2048,2048]{1,0:T(8,128)} %copy-done, f32[2048]{0:T(1024)S(1)} %bitcast.87, s32[2048]{0:T(1024)S(1)} %get-tuple-element.427, s32[2048]{0:T(1024)S(1)} %fusion.73, f32[1,1,2048,64]{2,3,1,0:T(8,128)S(1)} %get-tuple-element.412, bf16[16384,128]{0,1:T(8,128)(2,1)} %get-tuple-element.428, ...), kind=kOutput, calls=%fused_computation.8.clone.1 | convolution fusion | flops 562429952 | bytes 18120712 | tf_op jit(solution)/shard_map/while/body/eval_jaxpr/hgqk,khd->hgqd/dot_general | solution.py:84
  259.1 5.3 %fusion.75 = f32[2048]{0:T(1024)S(1)} fusion(f32[2048,2048]{1,0:T(8,128)S(1)} %get-tuple-element.393, f32[2048]{0:T(1024)S(1)} %bitcast.86, s32[2048]{0:T(1024)S(1)} %get-tuple-element.427, s32[2048]{0:T(1024)S(1)} %fusion.73), kind=kLoop, calls=%fused_computation.4.clone.1 | loop fusion | flops 25163776 | bytes 16809984 | tf_op jit(solution)/shard_map/while/body/eval_jaxpr/reduce_sum | solution.py:83
  264.8 8.1 %fusion.77 = f32[1,1,2048,64]{2,3,1,0:T(8,128)S(1)} fusion(f32[2048,2048]{1,0:T(8,128)} %copy-done, f32[2048]{0:T(1024)S(1)} %bitcast.87, s32[2048]{0:T(1024)S(1)} %get-tuple-element.427, s32[2048]{0:T(1024)S(1)} %fusion.73, f32[1,1,2048,64]{2,3,1,0:T(8,128)S(1)} %get-tuple-element.412, bf16[16384,128]{0,1:T(8,128)(2,1)} %get-tuple-element.428, ...), kind=kOutput, calls=%fused_computation.8.clone.1 | convolution fusion | flops 562429952 | bytes 18120712 | tf_op jit(solution)/shard_map/while/body/eval_jaxpr/hgqk,khd->hgqd/dot_general | solution.py:84
  276.8 5.3 %fusion.75 = f32[2048]{0:T(1024)S(1)} fusion(f32[2048,2048]{1,0:T(8,128)S(1)} %get-tuple-element.393, f32[2048]{0:T(1024)S(1)} %bitcast.86, s32[2048]{0:T(1024)S(1)} %get-tuple-element.427, s32[2048]{0:T(1024)S(1)} %fusion.73), kind=kLoop, calls=%fused_computation.4.clone.1 | loop fusion | flops 25163776 | bytes 16809984 | tf_op jit(solution)/shard_map/while/body/eval_jaxpr/reduce_sum | solution.py:83
  282.5 8.1 %fusion.77 = f32[1,1,2048,64]{2,3,1,0:T(8,128)S(1)} fusion(f32[2048,2048]{1,0:T(8,128)} %copy-done, f32[2048]{0:T(1024)S(1)} %bitcast.87, s32[2048]{0:T(1024)S(1)} %get-tuple-element.427, s32[2048]{0:T(1024)S(1)} %fusion.73, f32[1,1,2048,64]{2,3,1,0:T(8,128)S(1)} %get-tuple-element.412, bf16[16384,128]{0,1:T(8,128)(2,1)} %get-tuple-element.428, ...), kind=kOutput, calls=%fused_computation.8.clone.1 | convolution fusion | flops 562429952 | bytes 18120712 | tf_op jit(solution)/shard_map/while/body/eval_jaxpr/hgqk,khd->hgqd/dot_general | solution.py:84
  294.5 5.3 %fusion.75 = f32[2048]{0:T(1024)S(1)} fusion(f32[2048,2048]{1,0:T(8,128)S(1)} %get-tuple-element.393, f32[2048]{0:T(1024)S(1)} %bitcast.86, s32[2048]{0:T(1024)S(1)} %get-tuple-element.427, s32[2048]{0:T(1024)S(1)} %fusion.73), kind=kLoop, calls=%fused_computation.4.clone.1 | loop fusion | flops 25163776 | bytes 16809984 | tf_op jit(solution)/shard_map/while/body/eval_jaxpr/reduce_sum | solution.py:83
  300.2 8.1 %fusion.77 = f32[1,1,2048,64]{2,3,1,0:T(8,128)S(1)} fusion(f32[2048,2048]{1,0:T(8,128)} %copy-done, f32[2048]{0:T(1024)S(1)} %bitcast.87, s32[2048]{0:T(1024)S(1)} %get-tuple-element.427, s32[2048]{0:T(1024)S(1)} %fusion.73, f32[1,1,2048,64]{2,3,1,0:T(8,128)S(1)} %get-tuple-element.412, bf16[16384,128]{0,1:T(8,128)(2,1)} %get-tuple-element.428, ...), kind=kOutput, calls=%fused_computation.8.clone.1 | convolution fusion | flops 562429952 | bytes 18120712 | tf_op jit(solution)/shard_map/while/body/eval_jaxpr/hgqk,khd->hgqd/dot_general | solution.py:84
  312.2 5.3 %fusion.75 = f32[2048]{0:T(1024)S(1)} fusion(f32[2048,2048]{1,0:T(8,128)S(1)} %get-tuple-element.393, f32[2048]{0:T(1024)S(1)} %bitcast.86, s32[2048]{0:T(1024)S(1)} %get-tuple-element.427, s32[2048]{0:T(1024)S(1)} %fusion.73), kind=kLoop, calls=%fused_computation.4.clone.1 | loop fusion | flops 25163776 | bytes 16809984 | tf_op jit(solution)/shard_map/while/body/eval_jaxpr/reduce_sum | solution.py:83
  317.9 8.1 %fusion.77 = f32[1,1,2048,64]{2,3,1,0:T(8,128)S(1)} fusion(f32[2048,2048]{1,0:T(8,128)} %copy-done, f32[2048]{0:T(1024)S(1)} %bitcast.87, s32[2048]{0:T(1024)S(1)} %get-tuple-element.427, s32[2048]{0:T(1024)S(1)} %fusion.73, f32[1,1,2048,64]{2,3,1,0:T(8,128)S(1)} %get-tuple-element.412, bf16[16384,128]{0,1:T(8,128)(2,1)} %get-tuple-element.428, ...), kind=kOutput, calls=%fused_computation.8.clone.1 | convolution fusion | flops 562429952 | bytes 18120712 | tf_op jit(solution)/shard_map/while/body/eval_jaxpr/hgqk,khd->hgqd/dot_general | solution.py:84
  328.4 16.4 %all_to_all.16 = bf16[32,2,2048]{2,1,0:T(2,128)(2,1)S(1)} all-to-all(bf16[32,2,2048]{2,1,0:T(2,128)(2,1)S(1)} %reshape.437), channel_id=1, replica_groups=mesh['grp'=8,'sp'=32] {'sp'}, dimensions={0} | all-to-all | bytes 524288 | tf_op jit(solution)/shard_map/all_to_all | solution.py:146
  (114 shorter events, 43.9 us)
Async XLA Ops:
  6.5 5.1 %copy-start.1 = (s32[32]{0:T(128)S(1)}, s32[32]{0:T(128)}, u32[]{:S(2)}) copy-start(s32[32]{0:T(128)} %param.10) | copy-start | bytes 388
  6.5 61.1 %copy-start.2 = (bf16[2880,64]{0,1:T(8,128)(2,1)S(1)}, bf16[2880,64]{0,1:T(8,128)(2,1)}, u32[]{:S(2)}) copy-start(bf16[2880,64]{0,1:T(8,128)(2,1)} %param.8) | copy-start | bytes 1105924
  6.5 61.1 %all-gather.8.cloned.1.call-start = ((), (), s32[]{:S(2)}) async-start(), calls=%async_computation.2 | async-start | bytes 6217728 | tf_op jit(solution)/shard_map/all_gather | solution.py:26
  8.4 114.2 %all-gather.10.cloned.1.call-start = ((), (), s32[]{:S(2)}) async-start(), calls=%async_computation.3 | async-start | bytes 6217728 | tf_op jit(solution)/shard_map/all_gather | solution.py:26
  9.1 174.8 %all-gather.6.cloned.1.call-start = ((), (), s32[]{:S(2)}) async-start(), calls=%async_computation.1 | async-start | bytes 4718592 | tf_op jit(solution)/shard_map/all_gather | solution.py:131
  127.3 3.4 copy-start.3
  188.3 5.7 %copy-start = (f32[2048,2048]{1,0:T(8,128)}, f32[2048,2048]{1,0:T(8,128)S(1)}, u32[]{:S(2)}) copy-start(f32[2048,2048]{1,0:T(8,128)S(1)} %get-tuple-element.393) | copy-start | bytes 50331652 | tf_op jit(solution)/shard_map/while
  206.0 5.7 %copy-start = (f32[2048,2048]{1,0:T(8,128)}, f32[2048,2048]{1,0:T(8,128)S(1)}, u32[]{:S(2)}) copy-start(f32[2048,2048]{1,0:T(8,128)S(1)} %get-tuple-element.393) | copy-start | bytes 50331652 | tf_op jit(solution)/shard_map/while
  223.7 5.7 %copy-start = (f32[2048,2048]{1,0:T(8,128)}, f32[2048,2048]{1,0:T(8,128)S(1)}, u32[]{:S(2)}) copy-start(f32[2048,2048]{1,0:T(8,128)S(1)} %get-tuple-element.393) | copy-start | bytes 50331652 | tf_op jit(solution)/shard_map/while
  241.4 5.7 %copy-start = (f32[2048,2048]{1,0:T(8,128)}, f32[2048,2048]{1,0:T(8,128)S(1)}, u32[]{:S(2)}) copy-start(f32[2048,2048]{1,0:T(8,128)S(1)} %get-tuple-element.393) | copy-start | bytes 50331652 | tf_op jit(solution)/shard_map/while
  259.1 5.7 %copy-start = (f32[2048,2048]{1,0:T(8,128)}, f32[2048,2048]{1,0:T(8,128)S(1)}, u32[]{:S(2)}) copy-start(f32[2048,2048]{1,0:T(8,128)S(1)} %get-tuple-element.393) | copy-start | bytes 50331652 | tf_op jit(solution)/shard_map/while
  276.8 5.7 %copy-start = (f32[2048,2048]{1,0:T(8,128)}, f32[2048,2048]{1,0:T(8,128)S(1)}, u32[]{:S(2)}) copy-start(f32[2048,2048]{1,0:T(8,128)S(1)} %get-tuple-element.393) | copy-start | bytes 50331652 | tf_op jit(solution)/shard_map/while
  294.5 5.7 %copy-start = (f32[2048,2048]{1,0:T(8,128)}, f32[2048,2048]{1,0:T(8,128)S(1)}, u32[]{:S(2)}) copy-start(f32[2048,2048]{1,0:T(8,128)S(1)} %get-tuple-element.393) | copy-start | bytes 50331652 | tf_op jit(solution)/shard_map/while
  312.2 5.7 %copy-start = (f32[2048,2048]{1,0:T(8,128)}, f32[2048,2048]{1,0:T(8,128)S(1)}, u32[]{:S(2)}) copy-start(f32[2048,2048]{1,0:T(8,128)S(1)} %get-tuple-element.393) | copy-start | bytes 50331652 | tf_op jit(solution)/shard_map/while
Sparse Core Ops, SparseCore 0:
  9.9 57.7 all-gather.7
  70.2 52.4 all-gather.9
  130.8 53.0 all-gather.5
where the time goes:
time: 354 us; the launch traced here: 353 us
  waiting for transfers between devices  160 us (45%)
  matrix products  103 us (29%)
  other arithmetic  47.6 us (13%)
  blocking collectives  16.4 us (5%)
  between operations  13.3 us (4%)
  local copies, waits for them, and re-layouts  12.9 us (4%)
    all_gather x2, waiting for transfers between devices, piecewise(): finished.append(jax.vmap(apply)(lax.all_gather(share, axis), starts))  106 us
    dot_general x8, matrix products, attend(): jnp.einsum('hgqk,khd->hgqd', weights.astype(jnp.bfloat16), value_part, pr...  65 us
    all_gather x1, waiting for transfers between devices, per_device(): piece = lax.all_gather(key_value_pair, 'grp', axis=0, tiled=True)  52.6 us
    reduce_sum x8, other arithmetic, attend(): totals = totals * factor + jnp.sum(weights, axis=-1)  42.5 us
    dot_general x8, matrix products, attend(): jnp.einsum('qhgd,khd->hgqk', queries, key_part, preferred_element_type=jn...  28.7 us
    all_to_all x1, blocking collectives, per_device(): lax.all_to_all(attended, 'sp', split_axis=0, concat_axis=1, tiled=True)  16.4 us
    dot_general x2, matrix products, project(): return jnp.dot(piece, joined, preferred_element_type=jnp.float32)  9.01 us
  transfers between devices with their start and end apart: 3, of which 3 were waited for; matrix products, arithmetic and copies ran while one was open for 2% of the time, Pallas kernels for 0%

commit v1 on v0

--- a/solution.py
+++ b/solution.py
@@ -143,7 +143,10 @@
     maxima, totals, mixture = lax.fori_loop(0, turns, visit, initial)
     normed = jnp.transpose(mixture, (2, 0, 1, 3)) / jnp.transpose(totals, (2, 0, 1))[..., None]
     attended = normed.reshape(group_rows, query_cols).astype(jnp.bfloat16)
-    return lax.all_to_all(attended, "sp", split_axis=0, concat_axis=1, tiled=True)
+    return jnp.concatenate(
+        lax.all_to_all(jnp.stack(jnp.split(attended, lax.axis_size("sp"), axis=0)), "sp", 0, 0),
+        axis=1,
+    )
 
 
 def solution(mesh):

time: 354 us -> 326 us (0.921)
  matrix products: 103 us -> 78 us
    dot_general x8, matrix products: 65 us -> 40.4 us  [attend(): jnp.einsum('hgqk,khd->hgqd', weights.astype(jnp.bfloat16), value_part, pr...]
    while x26 -> x8, local copies, waits for them, and re-layouts: 3.98 us -> 0.02 us
where the time goes in v1:
time: 326 us; the launch traced here: 325 us
  waiting for transfers between devices  160 us (49%)
  matrix products  78 us (24%)
  other arithmetic  46.8 us (14%)
  blocking collectives  16.4 us (5%)
  between operations  13.4 us (4%)
  local copies, waits for them, and re-layouts  10.1 us (3%)
    all_gather x2, waiting for transfers between devices, piecewise(): finished.append(jax.vmap(apply)(lax.all_gather(share, axis), starts))  106 us
    all_gather x1, waiting for transfers between devices, per_device(): piece = lax.all_gather(key_value_pair, 'grp', axis=0, tiled=True)  52.5 us
    reduce_sum x8, other arithmetic, attend(): totals = totals * factor + jnp.sum(weights, axis=-1)  42.5 us
    dot_general x8, matrix products, attend(): jnp.einsum('hgqk,khd->hgqd', weights.astype(jnp.bfloat16), value_part, pr...  40.4 us
    dot_general x8, matrix products, attend(): jnp.einsum('qhgd,khd->hgqk', queries, key_part, preferred_element_type=jn...  28.6 us
    all_to_all x1, blocking collectives, per_device(): lax.all_to_all(jnp.stack(jnp.split(attended, lax.axis_size('sp'), axis=0)...  16.4 us
    dot_general x2, matrix products, project(): return jnp.dot(piece, joined, preferred_element_type=jnp.float32)  9.02 us
  transfers between devices with their start and end apart: 3, of which 3 were waited for; matrix products, arithmetic and copies ran while one was open for 2% of the time, Pallas kernels for 0%

profile of v1, /device:TPU:1, one launch (start us, length us, event | category | flops | bytes accessed | tf_op | source)
XLA Modules:
  0.0 325.0 jit_solution(11251660683940591663)
XLA Ops:
  11.8 55.8 %all-gather.10.cloned.1.call-done = bf16[1024,2880]{1,0:T(8,128)(2,1)} async-done(((bf16[32,2880]{1,0:T(8,128)(2,1)}), bf16[1024,2880]{1,0:T(8,128)(2,1)}) %all-gather.10.cloned.1.call-update) | async-done | bytes 5898256 | tf_op jit(solution)/shard_map/all_gather | solution.py:26
  67.6 4.5 %convolution_bitcast_fusion = f32[32,32,192]{2,1,0:T(8,128)S(1)} fusion(bf16[32,32,2880]{2,1,0:T(8,128)(2,1)} %bitcast.231, bf16[2880,64]{0,1:T(8,128)(2,1)S(1)} %copy.27, bf16[2880,64]{0,1:T(8,128)(2,1)S(1)} %copy.26, bf16[2880,64]{0,1:T(8,128)(2,1)S(1)} %copy-done.1), kind=kOutput, calls=%fused_computation.48 | convolution fusion | flops 1135779840 | bytes 7790592 | tf_op jit(solution)/shard_map/vmap()/dot_general | solution.py:113
  72.2 50.5 %all-gather.8.cloned.1.call-done = bf16[1024,2880]{1,0:T(8,128)(2,1)} async-done(((bf16[32,2880]{1,0:T(8,128)(2,1)}), bf16[1024,2880]{1,0:T(8,128)(2,1)}) %all-gather.8.cloned.1.call-update) | async-done | bytes 5898256 | tf_op jit(solution)/shard_map/all_gather | solution.py:26
  122.6 4.5 %convolution_bitcast_fusion.1 = f32[32,32,192]{2,1,0:T(8,128)S(1)} fusion(bf16[32,32,2880]{2,1,0:T(8,128)(2,1)} %bitcast.232, bf16[2880,64]{0,1:T(8,128)(2,1)S(1)} %copy.27, bf16[2880,64]{0,1:T(8,128)(2,1)S(1)} %copy.26, bf16[2880,64]{0,1:T(8,128)(2,1)S(1)} %copy-done.1), kind=kOutput, calls=%fused_computation.49 | convolution fusion | flops 1135779840 | bytes 7790592 | tf_op jit(solution)/shard_map/vmap()/dot_general | solution.py:113
  131.6 52.5 %all-gather.6.cloned.1.call-done = bf16[16384,128]{0,1:T(8,128)(2,1)} async-done(((bf16[2048,128]{0,1:T(8,128)(2,1)}), bf16[16384,128]{0,1:T(8,128)(2,1)}) %all-gather.6.cloned.1.call-update) | async-done | bytes 4194320 | tf_op jit(solution)/shard_map/all_gather | solution.py:131
  184.8 113.8 %while.21 = (s32[]{:T(128)}, f32[1,1,2048]{2,1,0:T(1,128)S(1)}, f32[1,1,2048]{2,1,0:T(1,128)S(1)}, f32[1,1,2048,64]{2,3,1,0:T(8,128)S(1)}, s32[32]{0:T(128)S(1)}...) while((s32[]{:T(128)}, f32[1,1,2048]{2,1,0:T(1,128)S(1)}, ...), condition=%wide.region_5.6_spmd.clone, body=%wide.region_1.5_spmd.clone.sunk | while | flops 1141592064 | bytes 52388188 | solution.py:143
  188.7 5.3 %fusion.76 = f32[2048]{0:T(1024)S(1)} fusion(f32[2048,2048]{1,0:T(8,128)S(1)} %get-tuple-element.377, f32[2048]{0:T(1024)S(1)} %bitcast.221, s32[2048]{0:T(1024)S(1)} %get-tuple-element.411, s32[2048]{0:T(1024)S(1)} %fusion.74), kind=kLoop, calls=%fused_computation.4.clone.1 | loop fusion | flops 25163776 | bytes 16809984 | tf_op jit(solution)/shard_map/while/body/eval_jaxpr/reduce_sum | solution.py:83
  194.0 5.0 %fusion.78 = f32[1,1,2048,64]{2,3,1,0:T(8,128)S(1)} fusion(f32[2048,2048]{1,0:T(8,128)S(1)} %get-tuple-element.377, f32[2048]{0:T(1024)S(1)} %bitcast.222, s32[2048]{0:T(1024)S(1)} %get-tuple-element.411, s32[2048]{0:T(1024)S(1)} %fusion.74, f32[1,1,2048,64]{2,3,1,0:T(8,128)S(1)} %get-tuple-element.396, bf16[16384,128]{0,1:T(8,128)(2,1)} %get-tuple-element.412, ...), kind=kOutput, calls=%fused_computation.8.clone.1 | convolution fusion | flops 562429952 | bytes 18120712 | tf_op jit(solution)/shard_map/while/body/eval_jaxpr/hgqk,khd->hgqd/dot_general | solution.py:84
  199.3 3.6 %fusion.75 = (f32[2048]{0:T(1024)S(1)}, f32[2048,2048]{1,0:T(8,128)S(1)}) fusion(s32[2048]{0:T(1024)S(1)} %get-tuple-element.411, s32[2048]{0:T(1024)S(1)} %fusion.74, bf16[2048,1,1,64]{0,3,2,1:T(8,128)(2,1)S(1)} %get-tuple-element.413, bf16[16384,128]{0,1:T(8,128)(2,1)} %get-tuple-element.412, s32[]{:T(128)S(6)} %select_n.248), kind=kOutput, calls=%fused_computation.2.clone.1 | convolution fusion | flops 553646080 | bytes 17326084 | tf_op jit(solution)/shard_map/while/body/eval_jaxpr/qhgd,khd->hgqk/dot_general | solution.py:75
  202.9 5.3 %fusion.76 = f32[2048]{0:T(1024)S(1)} fusion(f32[2048,2048]{1,0:T(8,128)S(1)} %get-tuple-element.377, f32[2048]{0:T(1024)S(1)} %bitcast.221, s32[2048]{0:T(1024)S(1)} %get-tuple-element.411, s32[2048]{0:T(1024)S(1)} %fusion.74), kind=kLoop, calls=%fused_computation.4.clone.1 | loop fusion | flops 25163776 | bytes 16809984 | tf_op jit(solution)/shard_map/while/body/eval_jaxpr/reduce_sum | solution.py:83
  208.2 5.0 %fusion.78 = f32[1,1,2048,64]{2,3,1,0:T(8,128)S(1)} fusion(f32[2048,2048]{1,0:T(8,128)S(1)} %get-tuple-element.377, f32[2048]{0:T(1024)S(1)} %bitcast.222, s32[2048]{0:T(1024)S(1)} %get-tuple-element.411, s32[2048]{0:T(1024)S(1)} %fusion.74, f32[1,1,2048,64]{2,3,1,0:T(8,128)S(1)} %get-tuple-element.396, bf16[16384,128]{0,1:T(8,128)(2,1)} %get-tuple-element.412, ...), kind=kOutput, calls=%fused_computation.8.clone.1 | convolution fusion | flops 562429952 | bytes 18120712 | tf_op jit(solution)/shard_map/while/body/eval_jaxpr/hgqk,khd->hgqd/dot_general | solution.py:84
  217.1 5.3 %fusion.76 = f32[2048]{0:T(1024)S(1)} fusion(f32[2048,2048]{1,0:T(8,128)S(1)} %get-tuple-element.377, f32[2048]{0:T(1024)S(1)} %bitcast.221, s32[2048]{0:T(1024)S(1)} %get-tuple-element.411, s32[2048]{0:T(1024)S(1)} %fusion.74), kind=kLoop, calls=%fused_computation.4.clone.1 | loop fusion | flops 25163776 | bytes 16809984 | tf_op jit(solution)/shard_map/while/body/eval_jaxpr/reduce_sum | solution.py:83
  222.5 5.0 %fusion.78 = f32[1,1,2048,64]{2,3,1,0:T(8,128)S(1)} fusion(f32[2048,2048]{1,0:T(8,128)S(1)} %get-tuple-element.377, f32[2048]{0:T(1024)S(1)} %bitcast.222, s32[2048]{0:T(1024)S(1)} %get-tuple-element.411, s32[2048]{0:T(1024)S(1)} %fusion.74, f32[1,1,2048,64]{2,3,1,0:T(8,128)S(1)} %get-tuple-element.396, bf16[16384,128]{0,1:T(8,128)(2,1)} %get-tuple-element.412, ...), kind=kOutput, calls=%fused_computation.8.clone.1 | convolution fusion | flops 562429952 | bytes 18120712 | tf_op jit(solution)/shard_map/while/body/eval_jaxpr/hgqk,khd->hgqd/dot_general | solution.py:84
  231.3 5.3 %fusion.76 = f32[2048]{0:T(1024)S(1)} fusion(f32[2048,2048]{1,0:T(8,128)S(1)} %get-tuple-element.377, f32[2048]{0:T(1024)S(1)} %bitcast.221, s32[2048]{0:T(1024)S(1)} %get-tuple-element.411, s32[2048]{0:T(1024)S(1)} %fusion.74), kind=kLoop, calls=%fused_computation.4.clone.1 | loop fusion | flops 25163776 | bytes 16809984 | tf_op jit(solution)/shard_map/while/body/eval_jaxpr/reduce_sum | solution.py:83
  236.7 5.0 %fusion.78 = f32[1,1,2048,64]{2,3,1,0:T(8,128)S(1)} fusion(f32[2048,2048]{1,0:T(8,128)S(1)} %get-tuple-element.377, f32[2048]{0:T(1024)S(1)} %bitcast.222, s32[2048]{0:T(1024)S(1)} %get-tuple-element.411, s32[2048]{0:T(1024)S(1)} %fusion.74, f32[1,1,2048,64]{2,3,1,0:T(8,128)S(1)} %get-tuple-element.396, bf16[16384,128]{0,1:T(8,128)(2,1)} %get-tuple-element.412, ...), kind=kOutput, calls=%fused_computation.8.clone.1 | convolution fusion | flops 562429952 | bytes 18120712 | tf_op jit(solution)/shard_map/while/body/eval_jaxpr/hgqk,khd->hgqd/dot_general | solution.py:84
  245.5 5.3 %fusion.76 = f32[2048]{0:T(1024)S(1)} fusion(f32[2048,2048]{1,0:T(8,128)S(1)} %get-tuple-element.377, f32[2048]{0:T(1024)S(1)} %bitcast.221, s32[2048]{0:T(1024)S(1)} %get-tuple-element.411, s32[2048]{0:T(1024)S(1)} %fusion.74), kind=kLoop, calls=%fused_computation.4.clone.1 | loop fusion | flops 25163776 | bytes 16809984 | tf_op jit(solution)/shard_map/while/body/eval_jaxpr/reduce_sum | solution.py:83
  250.9 5.0 %fusion.78 = f32[1,1,2048,64]{2,3,1,0:T(8,128)S(1)} fusion(f32[2048,2048]{1,0:T(8,128)S(1)} %get-tuple-element.377, f32[2048]{0:T(1024)S(1)} %bitcast.222, s32[2048]{0:T(1024)S(1)} %get-tuple-element.411, s32[2048]{0:T(1024)S(1)} %fusion.74, f32[1,1,2048,64]{2,3,1,0:T(8,128)S(1)} %get-tuple-element.396, bf16[16384,128]{0,1:T(8,128)(2,1)} %get-tuple-element.412, ...), kind=kOutput, calls=%fused_computation.8.clone.1 | convolution fusion | flops 562429952 | bytes 18120712 | tf_op jit(solution)/shard_map/while/body/eval_jaxpr/hgqk,khd->hgqd/dot_general | solution.py:84
  259.8 5.3 %fusion.76 = f32[2048]{0:T(1024)S(1)} fusion(f32[2048,2048]{1,0:T(8,128)S(1)} %get-tuple-element.377, f32[2048]{0:T(1024)S(1)} %bitcast.221, s32[2048]{0:T(1024)S(1)} %get-tuple-element.411, s32[2048]{0:T(1024)S(1)} %fusion.74), kind=kLoop, calls=%fused_computation.4.clone.1 | loop fusion | flops 25163776 | bytes 16809984 | tf_op jit(solution)/shard_map/while/body/eval_jaxpr/reduce_sum | solution.py:83
  265.1 5.0 %fusion.78 = f32[1,1,2048,64]{2,3,1,0:T(8,128)S(1)} fusion(f32[2048,2048]{1,0:T(8,128)S(1)} %get-tuple-element.377, f32[2048]{0:T(1024)S(1)} %bitcast.222, s32[2048]{0:T(1024)S(1)} %get-tuple-element.411, s32[2048]{0:T(1024)S(1)} %fusion.74, f32[1,1,2048,64]{2,3,1,0:T(8,128)S(1)} %get-tuple-element.396, bf16[16384,128]{0,1:T(8,128)(2,1)} %get-tuple-element.412, ...), kind=kOutput, calls=%fused_computation.8.clone.1 | convolution fusion | flops 562429952 | bytes 18120712 | tf_op jit(solution)/shard_map/while/body/eval_jaxpr/hgqk,khd->hgqd/dot_general | solution.py:84
  274.0 5.3 %fusion.76 = f32[2048]{0:T(1024)S(1)} fusion(f32[2048,2048]{1,0:T(8,128)S(1)} %get-tuple-element.377, f32[2048]{0:T(1024)S(1)} %bitcast.221, s32[2048]{0:T(1024)S(1)} %get-tuple-element.411, s32[2048]{0:T(1024)S(1)} %fusion.74), kind=kLoop, calls=%fused_computation.4.clone.1 | loop fusion | flops 25163776 | bytes 16809984 | tf_op jit(solution)/shard_map/while/body/eval_jaxpr/reduce_sum | solution.py:83
  279.3 5.0 %fusion.78 = f32[1,1,2048,64]{2,3,1,0:T(8,128)S(1)} fusion(f32[2048,2048]{1,0:T(8,128)S(1)} %get-tuple-element.377, f32[2048]{0:T(1024)S(1)} %bitcast.222, s32[2048]{0:T(1024)S(1)} %get-tuple-element.411, s32[2048]{0:T(1024)S(1)} %fusion.74, f32[1,1,2048,64]{2,3,1,0:T(8,128)S(1)} %get-tuple-element.396, bf16[16384,128]{0,1:T(8,128)(2,1)} %get-tuple-element.412, ...), kind=kOutput, calls=%fused_computation.8.clone.1 | convolution fusion | flops 562429952 | bytes 18120712 | tf_op jit(solution)/shard_map/while/body/eval_jaxpr/hgqk,khd->hgqd/dot_general | solution.py:84
  288.2 5.3 %fusion.76 = f32[2048]{0:T(1024)S(1)} fusion(f32[2048,2048]{1,0:T(8,128)S(1)} %get-tuple-element.377, f32[2048]{0:T(1024)S(1)} %bitcast.221, s32[2048]{0:T(1024)S(1)} %get-tuple-element.411, s32[2048]{0:T(1024)S(1)} %fusion.74), kind=kLoop, calls=%fused_computation.4.clone.1 | loop fusion | flops 25163776 | bytes 16809984 | tf_op jit(solution)/shard_map/while/body/eval_jaxpr/reduce_sum | solution.py:83
  293.6 5.0 %fusion.78 = f32[1,1,2048,64]{2,3,1,0:T(8,128)S(1)} fusion(f32[2048,2048]{1,0:T(8,128)S(1)} %get-tuple-element.377, f32[2048]{0:T(1024)S(1)} %bitcast.222, s32[2048]{0:T(1024)S(1)} %get-tuple-element.411, s32[2048]{0:T(1024)S(1)} %fusion.74, f32[1,1,2048,64]{2,3,1,0:T(8,128)S(1)} %get-tuple-element.396, bf16[16384,128]{0,1:T(8,128)(2,1)} %get-tuple-element.412, ...), kind=kOutput, calls=%fused_computation.8.clone.1 | convolution fusion | flops 562429952 | bytes 18120712 | tf_op jit(solution)/shard_map/while/body/eval_jaxpr/hgqk,khd->hgqd/dot_general | solution.py:84
  300.8 16.4 %all_to_all.5 = bf16[32,2,2048]{2,1,0:T(2,128)(2,1)S(1)} all-to-all(bf16[32,2,2048]{2,1,0:T(2,128)(2,1)S(1)} %reshape.431), channel_id=1, replica_groups=mesh['grp'=8,'sp'=32] {'sp'}, dimensions={0} | all-to-all | bytes 524288 | tf_op jit(solution)/shard_map/all_to_all | solution.py:147
  (125 shorter events, 40.3 us)
Async XLA Ops:
  6.5 5.1 %copy-start = (s32[32]{0:T(128)S(1)}, s32[32]{0:T(128)}, u32[]{:S(2)}) copy-start(s32[32]{0:T(128)} %param.10) | copy-start | bytes 388
  6.5 61.1 %copy-start.1 = (bf16[2880,64]{0,1:T(8,128)(2,1)S(1)}, bf16[2880,64]{0,1:T(8,128)(2,1)}, u32[]{:S(2)}) copy-start(bf16[2880,64]{0,1:T(8,128)(2,1)} %param.8) | copy-start | bytes 1105924
  6.5 61.1 %all-gather.10.cloned.1.call-start = ((), (), s32[]{:S(2)}) async-start(), calls=%async_computation.3 | async-start | bytes 6217728 | tf_op jit(solution)/shard_map/all_gather | solution.py:26
  8.4 114.2 %all-gather.8.cloned.1.call-start = ((), (), s32[]{:S(2)}) async-start(), calls=%async_computation.2 | async-start | bytes 6217728 | tf_op jit(solution)/shard_map/all_gather | solution.py:26
  9.1 175.0 %all-gather.6.cloned.1.call-start = ((), (), s32[]{:S(2)}) async-start(), calls=%async_computation.1 | async-start | bytes 4718592 | tf_op jit(solution)/shard_map/all_gather | solution.py:131
  127.4 3.5 %copy-start.2 = (f32[32]{0:T(128)S(1)}, f32[32]{0:T(128)}, u32[]{:S(2)}) copy-start(f32[32]{0:T(128)} %param.11) | copy-start | bytes 388
Sparse Core Ops, SparseCore 0:
  9.9 57.7 all-gather.9
  70.2 52.4 all-gather.7
  131.0 53.0 all-gather.5
